TPU v7x, 32 devices: a whole 2x2x4 slice. The times are simulated.
32 devices in a mesh: gx: 4 (over z), gy: 4 (over x, core), gz: 2 (over y).
Axes of the slice: x: 2, y: 2, z: 4, core: 2. Of those that a mesh axis runs over, the one named last changes fastest.
Arguments:
- coords: float32 [3, 4, 1024, 128], P(None, 'gx', ('gy', 'gz')), may hold values from 0 to 11
- charges: float32 [4, 1024, 128], P('gx', ('gy', 'gz')), may hold values from -1.5 to 1.5
- atom_types: int32 [4, 1024, 128], P('gx', ('gy', 'gz')), may hold values from 0 to 63
- lj_sigma: float32 [64], replicated, may hold values from 2 to 4
- lj_epsilon: float32 [64], replicated, may hold values from 0.02 to 0.25
- tile_list: int32 [4, 4, 2, 2, 512], P('gx', 'gy', 'gz'), may hold values from -1 to 3455, as said below
Outputs:
- forces: float32 [3, 4, 1024, 128], P(None, 'gx', ('gy', 'gz'))
Inputs may be any that keep to these rules, and one draw needn't show every extreme that they name: tile_list[x, y, z, 0, t] is a block of brick (x, y, z) (0 to 127) and tile_list[x, y, z, 1, t] a block of its neighbourhood whose cell touches the home block's cell or is that cell (cell indices differ by at most one along each dimension, counted across brick faces periodically); on each brick the listed tiles come first and the remaining slots hold -1 in both rows; at least 256 tiles are listed on every brick and all 512 on some brick; tiles may repeat.
All inputs are finite; a program needn't handle non-finite values.
Results may differ from a plain program's by a relative error of at most 0.0003.
Values sent between devices are 32-bit elements; how exact they have to be, the bound alone decides.
A program may use at most 128 MiB of HBM per device.

v0:
```python
import jax
import jax.numpy as jnp
from jax import lax
from jax.sharding import PartitionSpec as P

GRID = 4


cell_edge = 11.0
cutoff = 9.0
soft_core = 16.0
coulomb = 332.0636


def extended(block, sides, width):
    for axis, dim in sides:
        count = lax.axis_size(axis)
        forward = [(i, i + 1) for i in range(count - 1)]
        forward.append((count - 1, 0))
        backward = [(target, source) for source, target in forward]
        low = lax.ppermute(
            lax.slice_in_dim(block, block.shape[dim] - width, None, axis=dim), axis, forward
        )
        high = lax.ppermute(lax.slice_in_dim(block, 0, width, axis=dim), axis, backward)
        block = jnp.concatenate([low, block, high], axis=dim)
    return block


def radial(softened, sigma_pair, eps_pair, charge_pair):
    ratio = sigma_pair * sigma_pair / softened
    cubed = ratio * ratio * ratio
    return 24.0 * eps_pair * (2.0 * cubed * cubed - cubed) / softened + charge_pair / (
        softened * jnp.sqrt(softened)
    )


def tile_forces(home_block, source_block):
    delta = home_block[:3, :, :, None] - source_block[:3, :, None, :]
    dist_sq = jnp.sum(delta * delta, axis=0)
    softened = dist_sq + soft_core
    sigma_pair = 0.5 * (home_block[4][:, :, None] + source_block[4][:, None, :])
    eps_pair = home_block[5][:, :, None] * source_block[5][:, None, :]
    charge_pair = coulomb * home_block[3][:, :, None] * source_block[3][:, None, :]
    limit = jnp.full_like(softened, cutoff * cutoff + soft_core)
    shifted = radial(softened, sigma_pair, eps_pair, charge_pair) - radial(
        limit, sigma_pair, eps_pair, charge_pair
    )
    strength = jnp.where(dist_sq < cutoff * cutoff, shifted, jnp.zeros_like(shifted))
    return jnp.sum(strength[None] * delta, axis=3)


def brick_forces(home_atoms, region, tile_ids):
    count = tile_ids.shape[1]
    group = min(64, count)
    grouped = tile_ids.reshape(2, count // group, group).transpose(1, 0, 2)
    blocks = home_atoms.shape[1]
    rows = jnp.arange(blocks, dtype=jnp.int32)

    def advance(totals, pair_ids):
        home_block = jnp.take(home_atoms, jnp.maximum(pair_ids[0], 0), axis=1)
        source_block = jnp.take(region, jnp.maximum(pair_ids[1], 0), axis=1)
        pushes = tile_forces(home_block, source_block)
        selector = (pair_ids[0][None, :] == rows[:, None]).astype(totals.dtype)
        added = jnp.einsum("bg,cga->cba", selector, pushes, precision=lax.Precision.HIGHEST)
        return (totals + added, None)

    start = jnp.zeros((3,) + home_atoms.shape[1:], home_atoms.dtype)
    return lax.scan(advance, start, grouped)[0]


def cell_corners(dtype, grid, layers):
    block = jnp.arange(grid * grid * layers, dtype=jnp.int32)
    return (
        jnp.stack([block // (grid * layers), block // layers % grid, block % layers]).astype(dtype)
        * cell_edge
    )


def rim_shift(length, inner, dtype):
    index = jnp.arange(length + 2, dtype=jnp.int32)
    return ((index == length + 1).astype(jnp.int32) - (index == 0).astype(jnp.int32)).astype(
        dtype
    ) * (inner * cell_edge)


def per_device(coords, charges, atom_types, lj_sigma, lj_epsilon, tile_list):
    span_y = lax.axis_size("gy")
    span_z = lax.axis_size("gz")
    blocks = coords.shape[2]
    width = coords.shape[3]
    layers = blocks // (GRID * GRID)
    stride = blocks // (span_y * span_z)
    kinds = jnp.arange(lj_sigma.shape[0], dtype=jnp.int32)
    selector = (atom_types[0][:, :, None] == kinds).astype(coords.dtype)
    sigma_atom = jnp.sum(selector * lj_sigma, axis=2)
    root_atom = jnp.sum(selector * jnp.sqrt(lj_epsilon), axis=2)
    atoms = jnp.concatenate([coords[:, 0], charges, sigma_atom[None], root_atom[None]], 0)
    outgoing = atoms.reshape(6, stride, span_y * span_z, width)[:, None]
    arrived = lax.all_to_all(outgoing, ("gy", "gz"), split_axis=3, concat_axis=1, tiled=True)
    home_atoms = arrived.reshape(6, blocks, width)
    corners = cell_corners(coords.dtype, GRID, layers)
    home_atoms = jnp.concatenate([home_atoms[:3] + corners[:, :, None], home_atoms[3:]], 0)
    pairs = tile_list[0, 0, 0]
    cells = home_atoms.reshape(6, GRID, GRID, layers, width)
    padded = extended(cells, (("gx", 1), ("gy", 2), ("gz", 3)), 1)
    shift_x = rim_shift(GRID, GRID, coords.dtype)
    shift_y = rim_shift(GRID, GRID, coords.dtype)
    shift_z = rim_shift(layers, layers, coords.dtype)
    shape_pad = (GRID + 2, GRID + 2, layers + 2)
    shifts = jnp.stack(
        [
            jnp.broadcast_to(shift_x[:, None, None], shape_pad),
            jnp.broadcast_to(shift_y[None, :, None], shape_pad),
            jnp.broadcast_to(shift_z[None, None, :], shape_pad),
        ]
    )
    region = jnp.concatenate([padded[:3] + shifts[..., None], padded[3:]], 0)
    region = region.reshape(6, (GRID + 2) * (GRID + 2) * (layers + 2), width)
    source = jnp.maximum(pairs[1], 0)
    slot = source // blocks
    member = source % blocks
    place_x = member // (GRID * layers) + (slot // 9 - 1) * GRID + 1
    place_y = member // layers % GRID + (slot // 3 % 3 - 1) * GRID + 1
    place_z = member % layers + (slot % 3 - 1) * layers + 1
    placed = (place_x * (GRID + 2) + place_y) * (layers + 2) + place_z
    placed = jnp.where(pairs[1] < 0, 0, placed)
    pairs = jnp.stack([pairs[0], placed])
    totals = brick_forces(home_atoms, region, pairs)
    sending = totals.reshape(3, span_y * span_z, stride, width)[:, :, :, None]
    returned = lax.all_to_all(sending, ("gy", "gz"), split_axis=1, concat_axis=3, tiled=True)
    return returned.reshape(3, 1, blocks, width)


def solution(mesh):
    return jax.shard_map(
        per_device,
        mesh=mesh,
        in_specs=(
            P(None, "gx", ("gy", "gz"), None),
            P("gx", ("gy", "gz"), None),
            P("gx", ("gy", "gz"), None),
            P(),
            P(),
            P("gx", "gy", "gz", None, None),
        ),
        out_specs=P(None, "gx", ("gy", "gz"), None),
        check_vma=False,
    )
```

profile of v0, /device:TPU:0, one launch (start us, length us, event | category | flops | bytes accessed | tf_op | source)
XLA Modules:
  0.0 215.8 jit_solution(18356921924208487732)
XLA Ops:
  0.0 0.7 sqrt.10
  0.7 2.9 %select_reduce_fusion.1 = (f32[128,128]{1,0:T(8,128)S(1)}, f32[128,128]{1,0:T(8,128)S(1)}) fusion(f32[64]{0:T(128)} %param.11, s32[128,128]{1,0:T(8,128)} %bitcast.114, f32[64]{0:T(128)S(1)} %sqrt.10), kind=kLoop, calls=%fused_computation.40 | loop fusion | flops 5210112 | bytes 197120 | tf_op jit(solution)/shard_map/reduce_sum | solution.py:95
  3.6 1.0 pad_maximum_fusion.2
  4.6 0.8 copy.59
  5.4 5.2 %all-to-all-start = ((f32[6,1,16,8,128]{4,2,1,0,3:T(8,128)}), f32[6,1,16,8,128]{4,2,1,0,3:T(8,128)S(1)}, u32[]{:S(2)}, u32[]{:S(2)}) async-start(f32[6,1,16,8,128]{4,2,1,0,3:T(8,128)} %copy.59), calls=%async_computation | async-start | bytes 786432 | tf_op jit(solution)/shard_map/all_to_all | solution.py:99
  10.6 0.7 compare_reduce_fusion
  11.3 0.8 slice_reduce_fusion
  12.8 5.2 %all-to-all-done = f32[6,1,16,8,128]{4,2,1,0,3:T(8,128)S(1)} async-done(((f32[6,1,16,8,128]{4,2,1,0,3:T(8,128)}), f32[6,1,16,8,128]{4,2,1,0,3:T(8,128)S(1)}, u32[]{:S(2)}, u32[]{:S(2)}) %all-to-all-start) | async-done | bytes 393248 | tf_op jit(solution)/shard_map/all_to_all | solution.py:99
  18.2 1.6 collective-permute-start
  19.8 2.2 %collective-permute-start.1 = (f32[6,1,4,8,128]{4,3,2,1,0:T(8,128)S(1)}, f32[6,1,4,8,128]{4,3,2,1,0:T(8,128)S(1)}, u32[]{:S(2)}, u32[]{:S(2)}) collective-permute-start(f32[6,1,4,8,128]{4,3,2,1,0:T(8,128)S(1)} %get-tuple-element.118), channel_id=1, source_target_pairs={{8,0},{16,8},{24,16},{0,24},{9,1},{17,9},{25,17},{1,25},{10,2},{18... | collective-permute-start | bytes 294920 | tf_op jit(solution)/shard_map/ppermute | solution.py:24
  22.1 3.6 %collective-permute-done = f32[6,1,4,8,128]{4,3,2,1,0:T(8,128)S(1)} collective-permute-done((f32[6,1,4,8,128]{4,3,2,1,0:T(8,128)S(1)}, f32[6,1,4,8,128]{4,3,2,1,0:T(8,128)S(1)}, u32[]{:S(2)}, u32[]{:S(2)}) %collective-permute-start) | collective-permute-done | bytes 98336 | tf_op jit(solution)/shard_map/ppermute | solution.py:21
  25.7 0.9 collective-permute-done.1
  26.6 1.7 collective-permute-start.3
  28.5 2.7 %collective-permute-done.2 = f32[6,6,1,8,128]{4,3,2,1,0:T(8,128)S(1)} collective-permute-done((f32[6,6,1,8,128]{4,3,2,1,0:T(8,128)S(1)}, f32[6,6,1,8,128]{4,3,2,1,0:T(8,128)S(1)}, u32[]{:S(2)}, u32[]{:S(2)}) %collective-permute-start.2) | collective-permute-done | bytes 147488 | tf_op jit(solution)/shard_map/ppermute | solution.py:21
  31.8 0.8 collective-permute-start.4
  32.6 1.3 collective-permute-start.5
  34.1 3.6 %collective-permute-done.4 = f32[6,6,6,1,128]{4,3,2,1,0:T(1,128)S(1)} collective-permute-done((f32[6,6,6,1,128]{4,3,2,1,0:T(1,128)S(1)}, f32[6,6,6,1,128]{4,3,2,1,0:T(1,128)S(1)}, u32[]{:S(2)}, u32[]{:S(2)}) %collective-permute-start.4) | collective-permute-done | bytes 110624 | tf_op jit(solution)/shard_map/ppermute | solution.py:21
  37.7 2.4 %collective-permute-done.5 = f32[6,6,6,1,128]{4,3,2,1,0:T(1,128)S(1)} collective-permute-done((f32[6,6,6,1,128]{4,3,2,1,0:T(1,128)S(1)}, f32[6,6,6,1,128]{4,3,2,1,0:T(1,128)S(1)}, u32[]{:S(2)}, u32[]{:S(2)}) %collective-permute-start.5) | collective-permute-done | bytes 110624 | tf_op jit(solution)/shard_map/ppermute | solution.py:24
  41.0 0.7 copy.61
  41.6 165.6 %while.11 = (s32[]{:T(128)}, f32[3,128,128]{1,2,0:T(8,128)S(1)}, s32[8,2,64]{2,0,1:T(8,128)S(1)}, f32[6,128,128]{2,0,1:T(8,128)S(1)}, f32[6,360,128]{2,0,1:T(8,128)S(1)}, /*index=5*/s32[]{:T(128)}, s32[]{:T(128)}) while((s32[]{:T(128)}, f32[3,128,128]{1,2,0:T(8,128)S(1)}, s32[8,2,64]{2,0,1:T(8,128)S(1)}, ...), condition=%wide.region_5.6_spmd.clone, body=%wide.region_2.5_spmd.clone.sunk | while | flops 88271232 | bytes 20722016 | solution.py:68
  41.7 0.6 gather_fusion
  42.6 0.6 gather_fusion.1
  43.6 4.1 %fusion.68 = f32[64,128,128]{2,1,0:T(8,128)S(1)} fusion(f32[3,64,128]{2,1,0:T(8,128)S(1)} %copy.75, f32[3,64,128]{2,1,0:T(8,128)S(1)} %copy.76), kind=kLoop, calls=%fused_computation.5.clone.1 | loop fusion | flops 8388608 | bytes 4390912 | tf_op jit(solution)/shard_map/while/body/eval_jaxpr/reduce_sum | solution.py:39
  47.7 6.5 %fusion.71 = f32[64,128,128]{2,1,0:T(8,128)S(1)} fusion(f32[64,128,128]{2,1,0:T(8,128)S(1)} %fusion.68, f32[64,128]{1,0:T(8,128)S(1)} %bitcast.99, f32[64,128]{1,0:T(8,128)S(1)} %bitcast.102, f32[64,128]{1,0:T(8,128)S(1)} %bitcast.100, f32[64,128]{1,0:T(8,128)S(1)} %bitcast.103, f32[64,128]{1,0:T(8,128)S(1)} %bitcast.98, f32[64,128]{1,0:T(8,128)S(1)} %bitcast.101), kind=kLoop, calls=%fused_computation.16.clone.1 | loop fusion | flops 32505856 | bytes 8585216 | tf_op jit(solution)/shard_map/while/body/eval_jaxpr/jit(_where)/select_n | solution.py:48
  54.3 7.7 %fusion.72 = f32[3,64,128]{2,1,0:T(8,128)S(1)} fusion(f32[64,128,128]{2,1,0:T(8,128)S(1)} %fusion.71, f32[3,64,128]{2,1,0:T(8,128)S(1)} %copy.75, f32[3,64,128]{2,1,0:T(8,128)S(1)} %copy.76), kind=kLoop, calls=%fused_computation.6.clone.1 | loop fusion | flops 9412608 | bytes 4489216 | tf_op jit(solution)/shard_map/while/body/eval_jaxpr/reduce_sum | solution.py:49
  64.3 4.1 %fusion.68 = f32[64,128,128]{2,1,0:T(8,128)S(1)} fusion(f32[3,64,128]{2,1,0:T(8,128)S(1)} %copy.75, f32[3,64,128]{2,1,0:T(8,128)S(1)} %copy.76), kind=kLoop, calls=%fused_computation.5.clone.1 | loop fusion | flops 8388608 | bytes 4390912 | tf_op jit(solution)/shard_map/while/body/eval_jaxpr/reduce_sum | solution.py:39
  68.4 6.5 %fusion.71 = f32[64,128,128]{2,1,0:T(8,128)S(1)} fusion(f32[64,128,128]{2,1,0:T(8,128)S(1)} %fusion.68, f32[64,128]{1,0:T(8,128)S(1)} %bitcast.99, f32[64,128]{1,0:T(8,128)S(1)} %bitcast.102, f32[64,128]{1,0:T(8,128)S(1)} %bitcast.100, f32[64,128]{1,0:T(8,128)S(1)} %bitcast.103, f32[64,128]{1,0:T(8,128)S(1)} %bitcast.98, f32[64,128]{1,0:T(8,128)S(1)} %bitcast.101), kind=kLoop, calls=%fused_computation.16.clone.1 | loop fusion | flops 32505856 | bytes 8585216 | tf_op jit(solution)/shard_map/while/body/eval_jaxpr/jit(_where)/select_n | solution.py:48
  75.0 7.7 %fusion.72 = f32[3,64,128]{2,1,0:T(8,128)S(1)} fusion(f32[64,128,128]{2,1,0:T(8,128)S(1)} %fusion.71, f32[3,64,128]{2,1,0:T(8,128)S(1)} %copy.75, f32[3,64,128]{2,1,0:T(8,128)S(1)} %copy.76), kind=kLoop, calls=%fused_computation.6.clone.1 | loop fusion | flops 9412608 | bytes 4489216 | tf_op jit(solution)/shard_map/while/body/eval_jaxpr/reduce_sum | solution.py:49
  85.0 4.1 %fusion.68 = f32[64,128,128]{2,1,0:T(8,128)S(1)} fusion(f32[3,64,128]{2,1,0:T(8,128)S(1)} %copy.75, f32[3,64,128]{2,1,0:T(8,128)S(1)} %copy.76), kind=kLoop, calls=%fused_computation.5.clone.1 | loop fusion | flops 8388608 | bytes 4390912 | tf_op jit(solution)/shard_map/while/body/eval_jaxpr/reduce_sum | solution.py:39
  89.1 6.5 %fusion.71 = f32[64,128,128]{2,1,0:T(8,128)S(1)} fusion(f32[64,128,128]{2,1,0:T(8,128)S(1)} %fusion.68, f32[64,128]{1,0:T(8,128)S(1)} %bitcast.99, f32[64,128]{1,0:T(8,128)S(1)} %bitcast.102, f32[64,128]{1,0:T(8,128)S(1)} %bitcast.100, f32[64,128]{1,0:T(8,128)S(1)} %bitcast.103, f32[64,128]{1,0:T(8,128)S(1)} %bitcast.98, f32[64,128]{1,0:T(8,128)S(1)} %bitcast.101), kind=kLoop, calls=%fused_computation.16.clone.1 | loop fusion | flops 32505856 | bytes 8585216 | tf_op jit(solution)/shard_map/while/body/eval_jaxpr/jit(_where)/select_n | solution.py:48
  95.6 7.7 %fusion.72 = f32[3,64,128]{2,1,0:T(8,128)S(1)} fusion(f32[64,128,128]{2,1,0:T(8,128)S(1)} %fusion.71, f32[3,64,128]{2,1,0:T(8,128)S(1)} %copy.75, f32[3,64,128]{2,1,0:T(8,128)S(1)} %copy.76), kind=kLoop, calls=%fused_computation.6.clone.1 | loop fusion | flops 9412608 | bytes 4489216 | tf_op jit(solution)/shard_map/while/body/eval_jaxpr/reduce_sum | solution.py:49
  105.6 4.1 %fusion.68 = f32[64,128,128]{2,1,0:T(8,128)S(1)} fusion(f32[3,64,128]{2,1,0:T(8,128)S(1)} %copy.75, f32[3,64,128]{2,1,0:T(8,128)S(1)} %copy.76), kind=kLoop, calls=%fused_computation.5.clone.1 | loop fusion | flops 8388608 | bytes 4390912 | tf_op jit(solution)/shard_map/while/body/eval_jaxpr/reduce_sum | solution.py:39
  109.8 6.5 %fusion.71 = f32[64,128,128]{2,1,0:T(8,128)S(1)} fusion(f32[64,128,128]{2,1,0:T(8,128)S(1)} %fusion.68, f32[64,128]{1,0:T(8,128)S(1)} %bitcast.99, f32[64,128]{1,0:T(8,128)S(1)} %bitcast.102, f32[64,128]{1,0:T(8,128)S(1)} %bitcast.100, f32[64,128]{1,0:T(8,128)S(1)} %bitcast.103, f32[64,128]{1,0:T(8,128)S(1)} %bitcast.98, f32[64,128]{1,0:T(8,128)S(1)} %bitcast.101), kind=kLoop, calls=%fused_computation.16.clone.1 | loop fusion | flops 32505856 | bytes 8585216 | tf_op jit(solution)/shard_map/while/body/eval_jaxpr/jit(_where)/select_n | solution.py:48
  116.3 7.7 %fusion.72 = f32[3,64,128]{2,1,0:T(8,128)S(1)} fusion(f32[64,128,128]{2,1,0:T(8,128)S(1)} %fusion.71, f32[3,64,128]{2,1,0:T(8,128)S(1)} %copy.75, f32[3,64,128]{2,1,0:T(8,128)S(1)} %copy.76), kind=kLoop, calls=%fused_computation.6.clone.1 | loop fusion | flops 9412608 | bytes 4489216 | tf_op jit(solution)/shard_map/while/body/eval_jaxpr/reduce_sum | solution.py:49
  126.3 4.1 %fusion.68 = f32[64,128,128]{2,1,0:T(8,128)S(1)} fusion(f32[3,64,128]{2,1,0:T(8,128)S(1)} %copy.75, f32[3,64,128]{2,1,0:T(8,128)S(1)} %copy.76), kind=kLoop, calls=%fused_computation.5.clone.1 | loop fusion | flops 8388608 | bytes 4390912 | tf_op jit(solution)/shard_map/while/body/eval_jaxpr/reduce_sum | solution.py:39
  130.5 6.5 %fusion.71 = f32[64,128,128]{2,1,0:T(8,128)S(1)} fusion(f32[64,128,128]{2,1,0:T(8,128)S(1)} %fusion.68, f32[64,128]{1,0:T(8,128)S(1)} %bitcast.99, f32[64,128]{1,0:T(8,128)S(1)} %bitcast.102, f32[64,128]{1,0:T(8,128)S(1)} %bitcast.100, f32[64,128]{1,0:T(8,128)S(1)} %bitcast.103, f32[64,128]{1,0:T(8,128)S(1)} %bitcast.98, f32[64,128]{1,0:T(8,128)S(1)} %bitcast.101), kind=kLoop, calls=%fused_computation.16.clone.1 | loop fusion | flops 32505856 | bytes 8585216 | tf_op jit(solution)/shard_map/while/body/eval_jaxpr/jit(_where)/select_n | solution.py:48
  137.0 7.7 %fusion.72 = f32[3,64,128]{2,1,0:T(8,128)S(1)} fusion(f32[64,128,128]{2,1,0:T(8,128)S(1)} %fusion.71, f32[3,64,128]{2,1,0:T(8,128)S(1)} %copy.75, f32[3,64,128]{2,1,0:T(8,128)S(1)} %copy.76), kind=kLoop, calls=%fused_computation.6.clone.1 | loop fusion | flops 9412608 | bytes 4489216 | tf_op jit(solution)/shard_map/while/body/eval_jaxpr/reduce_sum | solution.py:49
  147.0 4.1 %fusion.68 = f32[64,128,128]{2,1,0:T(8,128)S(1)} fusion(f32[3,64,128]{2,1,0:T(8,128)S(1)} %copy.75, f32[3,64,128]{2,1,0:T(8,128)S(1)} %copy.76), kind=kLoop, calls=%fused_computation.5.clone.1 | loop fusion | flops 8388608 | bytes 4390912 | tf_op jit(solution)/shard_map/while/body/eval_jaxpr/reduce_sum | solution.py:39
  151.2 6.5 %fusion.71 = f32[64,128,128]{2,1,0:T(8,128)S(1)} fusion(f32[64,128,128]{2,1,0:T(8,128)S(1)} %fusion.68, f32[64,128]{1,0:T(8,128)S(1)} %bitcast.99, f32[64,128]{1,0:T(8,128)S(1)} %bitcast.102, f32[64,128]{1,0:T(8,128)S(1)} %bitcast.100, f32[64,128]{1,0:T(8,128)S(1)} %bitcast.103, f32[64,128]{1,0:T(8,128)S(1)} %bitcast.98, f32[64,128]{1,0:T(8,128)S(1)} %bitcast.101), kind=kLoop, calls=%fused_computation.16.clone.1 | loop fusion | flops 32505856 | bytes 8585216 | tf_op jit(solution)/shard_map/while/body/eval_jaxpr/jit(_where)/select_n | solution.py:48
  157.7 7.7 %fusion.72 = f32[3,64,128]{2,1,0:T(8,128)S(1)} fusion(f32[64,128,128]{2,1,0:T(8,128)S(1)} %fusion.71, f32[3,64,128]{2,1,0:T(8,128)S(1)} %copy.75, f32[3,64,128]{2,1,0:T(8,128)S(1)} %copy.76), kind=kLoop, calls=%fused_computation.6.clone.1 | loop fusion | flops 9412608 | bytes 4489216 | tf_op jit(solution)/shard_map/while/body/eval_jaxpr/reduce_sum | solution.py:49
  167.7 4.1 %fusion.68 = f32[64,128,128]{2,1,0:T(8,128)S(1)} fusion(f32[3,64,128]{2,1,0:T(8,128)S(1)} %copy.75, f32[3,64,128]{2,1,0:T(8,128)S(1)} %copy.76), kind=kLoop, calls=%fused_computation.5.clone.1 | loop fusion | flops 8388608 | bytes 4390912 | tf_op jit(solution)/shard_map/while/body/eval_jaxpr/reduce_sum | solution.py:39
  171.9 6.5 %fusion.71 = f32[64,128,128]{2,1,0:T(8,128)S(1)} fusion(f32[64,128,128]{2,1,0:T(8,128)S(1)} %fusion.68, f32[64,128]{1,0:T(8,128)S(1)} %bitcast.99, f32[64,128]{1,0:T(8,128)S(1)} %bitcast.102, f32[64,128]{1,0:T(8,128)S(1)} %bitcast.100, f32[64,128]{1,0:T(8,128)S(1)} %bitcast.103, f32[64,128]{1,0:T(8,128)S(1)} %bitcast.98, f32[64,128]{1,0:T(8,128)S(1)} %bitcast.101), kind=kLoop, calls=%fused_computation.16.clone.1 | loop fusion | flops 32505856 | bytes 8585216 | tf_op jit(solution)/shard_map/while/body/eval_jaxpr/jit(_where)/select_n | solution.py:48
  178.4 7.7 %fusion.72 = f32[3,64,128]{2,1,0:T(8,128)S(1)} fusion(f32[64,128,128]{2,1,0:T(8,128)S(1)} %fusion.71, f32[3,64,128]{2,1,0:T(8,128)S(1)} %copy.75, f32[3,64,128]{2,1,0:T(8,128)S(1)} %copy.76), kind=kLoop, calls=%fused_computation.6.clone.1 | loop fusion | flops 9412608 | bytes 4489216 | tf_op jit(solution)/shard_map/while/body/eval_jaxpr/reduce_sum | solution.py:49
  188.4 4.1 %fusion.68 = f32[64,128,128]{2,1,0:T(8,128)S(1)} fusion(f32[3,64,128]{2,1,0:T(8,128)S(1)} %copy.75, f32[3,64,128]{2,1,0:T(8,128)S(1)} %copy.76), kind=kLoop, calls=%fused_computation.5.clone.1 | loop fusion | flops 8388608 | bytes 4390912 | tf_op jit(solution)/shard_map/while/body/eval_jaxpr/reduce_sum | solution.py:39
  192.6 6.5 %fusion.71 = f32[64,128,128]{2,1,0:T(8,128)S(1)} fusion(f32[64,128,128]{2,1,0:T(8,128)S(1)} %fusion.68, f32[64,128]{1,0:T(8,128)S(1)} %bitcast.99, f32[64,128]{1,0:T(8,128)S(1)} %bitcast.102, f32[64,128]{1,0:T(8,128)S(1)} %bitcast.100, f32[64,128]{1,0:T(8,128)S(1)} %bitcast.103, f32[64,128]{1,0:T(8,128)S(1)} %bitcast.98, f32[64,128]{1,0:T(8,128)S(1)} %bitcast.101), kind=kLoop, calls=%fused_computation.16.clone.1 | loop fusion | flops 32505856 | bytes 8585216 | tf_op jit(solution)/shard_map/while/body/eval_jaxpr/jit(_where)/select_n | solution.py:48
  199.1 7.7 %fusion.72 = f32[3,64,128]{2,1,0:T(8,128)S(1)} fusion(f32[64,128,128]{2,1,0:T(8,128)S(1)} %fusion.71, f32[3,64,128]{2,1,0:T(8,128)S(1)} %copy.75, f32[3,64,128]{2,1,0:T(8,128)S(1)} %copy.76), kind=kLoop, calls=%fused_computation.6.clone.1 | loop fusion | flops 9412608 | bytes 4489216 | tf_op jit(solution)/shard_map/while/body/eval_jaxpr/reduce_sum | solution.py:49
  207.3 7.8 %all_to_all.30 = f32[3,8,16,1,128]{4,2,0,3,1:T(8,128)S(1)} all-to-all(f32[3,8,16,1,128]{4,2,0,3,1:T(8,128)S(1)} %copy.65), channel_id=1, replica_groups=mesh['gx'=4,'gy'=4,'gz'=2] {'gy','gz'}, dimensions={1} | all-to-all | bytes 393216 | tf_op jit(solution)/shard_map/all_to_all | solution.py:130
  215.1 0.7 copy.72
  (162 shorter events, 19.2 us)
Async XLA Ops:
  5.4 12.6 %all-to-all-start = ((f32[6,1,16,8,128]{4,2,1,0,3:T(8,128)}), f32[6,1,16,8,128]{4,2,1,0,3:T(8,128)S(1)}, u32[]{:S(2)}, u32[]{:S(2)}) async-start(f32[6,1,16,8,128]{4,2,1,0,3:T(8,128)} %copy.59), calls=%async_computation | async-start | bytes 786432 | tf_op jit(solution)/shard_map/all_to_all | solution.py:99
  18.2 7.4 %collective-permute-start = (f32[6,1,4,8,128]{4,3,2,1,0:T(8,128)S(1)}, f32[6,1,4,8,128]{4,3,2,1,0:T(8,128)S(1)}, u32[]{:S(2)}, u32[]{:S(2)}) collective-permute-start(f32[6,1,4,8,128]{4,3,2,1,0:T(8,128)S(1)} %get-tuple-element.117), channel_id=1, source_target_pairs={{0,8},{8,16},{16,24},{24,0},{1,9},{9,17},{17,25},{25,1},{2,10},{10... | collective-permute-start | bytes 294920 | tf_op jit(solution)/shard_map/ppermute | solution.py:21
  19.8 6.7 %collective-permute-start.1 = (f32[6,1,4,8,128]{4,3,2,1,0:T(8,128)S(1)}, f32[6,1,4,8,128]{4,3,2,1,0:T(8,128)S(1)}, u32[]{:S(2)}, u32[]{:S(2)}) collective-permute-start(f32[6,1,4,8,128]{4,3,2,1,0:T(8,128)S(1)} %get-tuple-element.118), channel_id=1, source_target_pairs={{8,0},{16,8},{24,16},{0,24},{9,1},{17,9},{25,17},{1,25},{10,2},{18... | collective-permute-start | bytes 294920 | tf_op jit(solution)/shard_map/ppermute | solution.py:24
  26.6 4.6 %collective-permute-start.2 = (f32[6,6,1,8,128]{4,3,2,1,0:T(8,128)S(1)}, f32[6,6,1,8,128]{4,3,2,1,0:T(8,128)S(1)}, u32[]{:S(2)}, u32[]{:S(2)}) collective-permute-start(f32[6,6,1,8,128]{4,3,2,1,0:T(8,128)S(1)} %get-tuple-element.115), channel_id=1, source_target_pairs={{0,2},{2,4},{4,6},{6,0},{1,3},{3,5},{5,7},{7,1},{8,10},{10,12},{12... | collective-permute-start | bytes 442376 | tf_op jit(solution)/shard_map/ppermute | solution.py:21
  26.6 5.0 %collective-permute-start.3 = (f32[6,6,1,8,128]{4,3,2,1,0:T(8,128)S(1)}, f32[6,6,1,8,128]{4,3,2,1,0:T(8,128)S(1)}, u32[]{:S(2)}, u32[]{:S(2)}) collective-permute-start(f32[6,6,1,8,128]{4,3,2,1,0:T(8,128)S(1)} %get-tuple-element.116), channel_id=1, source_target_pairs={{2,0},{4,2},{6,4},{0,6},{3,1},{5,3},{7,5},{1,7},{10,8},{12,10},{14... | collective-permute-start | bytes 442376 | tf_op jit(solution)/shard_map/ppermute | solution.py:24
  31.8 5.9 %collective-permute-start.4 = (f32[6,6,6,1,128]{4,3,2,1,0:T(1,128)S(1)}, f32[6,6,6,1,128]{4,3,2,1,0:T(1,128)S(1)}, u32[]{:S(2)}, u32[]{:S(2)}) collective-permute-start(f32[6,6,6,1,128]{4,3,2,1,0:T(1,128)S(1)} %get-tuple-element.113), channel_id=1, source_target_pairs={{0,1},{1,0},{2,3},{3,2},{4,5},{5,4},{6,7},{7,6},{8,9},{9,8},{10,11... | collective-permute-start | bytes 331784 | tf_op jit(solution)/shard_map/ppermute | solution.py:21
  32.6 7.5 %collective-permute-start.5 = (f32[6,6,6,1,128]{4,3,2,1,0:T(1,128)S(1)}, f32[6,6,6,1,128]{4,3,2,1,0:T(1,128)S(1)}, u32[]{:S(2)}, u32[]{:S(2)}) collective-permute-start(f32[6,6,6,1,128]{4,3,2,1,0:T(1,128)S(1)} %get-tuple-element.114), channel_id=1, source_target_pairs={{1,0},{0,1},{3,2},{2,3},{5,4},{4,5},{7,6},{6,7},{9,8},{8,9},{11,10... | collective-permute-start | bytes 331784 | tf_op jit(solution)/shard_map/ppermute | solution.py:24
where the time goes:
time: 216 us
  other arithmetic  157 us (73%)
  waiting for transfers between devices  18.7 us (9%)
  local copies, waits for them, and re-layouts  15.2 us (7%)
  starting transfers between devices  13 us (6%)
  blocking collectives  7.76 us (4%)
  matrix products  3.16 us (1%)
    reduce_sum x8, other arithmetic, tile_forces(): return jnp.sum(strength[None] * delta, axis=3)  61.2 us
    select_n x8, other arithmetic, tile_forces(): jnp.where(dist_sq < cutoff * cutoff, shifted, jnp.zeros_like(shifted))  52.3 us
    reduce_sum x8, other arithmetic, tile_forces(): dist_sq = jnp.sum(delta * delta, axis=0)  33.1 us
    ppermute x3, waiting for transfers between devices, extended(): lax.ppermute(lax.slice_in_dim(block, block.shape[dim] - width, None, axis...  9.84 us
    all_to_all x1, blocking collectives, per_device(): lax.all_to_all(sending, ('gy', 'gz'), split_axis=1, concat_axis=3, tiled=...  7.76 us
    ppermute x3, starting transfers between devices, extended(): lax.ppermute(lax.slice_in_dim(block, 0, width, axis=dim), axis, backward)  5.25 us
    all_to_all x1, starting transfers between devices, per_device(): lax.all_to_all(outgoing, ('gy', 'gz'), split_axis=3, concat_axis=1, tiled...  5.2 us
    all_to_all x1, waiting for transfers between devices, per_device(): lax.all_to_all(outgoing, ('gy', 'gz'), split_axis=3, concat_axis=1, tiled...  5.15 us
  transfers between devices with their start and end apart: 7, of which 7 were waited for; matrix products, arithmetic and copies ran while one was open for 1% of the time, Pallas kernels for 0%

commit v1 on v0

v1 whole, which is shorter than its diff:
```python
import functools

import jax
import jax.numpy as jnp
from jax import lax
from jax.experimental import pallas as pl
from jax.experimental.pallas import tpu as pltpu
from jax.sharding import PartitionSpec as P

GRID = 4
ROWS = 8

cell_edge = 11.0
cutoff = 9.0
soft_core = 16.0
coulomb = 332.0636
limit = cutoff * cutoff + soft_core
sigma_scale = 0.5 * 2.0 ** (1.0 / 6.0)
root_scale = 12.0**0.5
charge_scale = coulomb**0.5


def extended(block, sides, width):
    for axis, dim in sides:
        count = lax.axis_size(axis)
        forward = [(i, i + 1) for i in range(count - 1)]
        forward.append((count - 1, 0))
        backward = [(target, source) for source, target in forward]
        low = lax.ppermute(
            lax.slice_in_dim(block, block.shape[dim] - width, None, axis=dim), axis, forward
        )
        high = lax.ppermute(lax.slice_in_dim(block, 0, width, axis=dim), axis, backward)
        block = jnp.concatenate([low, block, high], axis=dim)
    return block


def powers(softened):
    root = lax.rsqrt(softened)
    one = root * root
    two = one * one
    four = two * two
    return one * root, four, four * (two * one)


def force_kernel(pairs, count, region, out, totals):
    width = region.shape[2]
    half, four_at, seven_at = powers(jnp.full((8, width), limit, jnp.float32))

    totals[...] = jnp.zeros_like(totals)

    def tile(index):
        home = pairs[1, index]
        source = region[pairs[2, index]].T
        mine = [jnp.broadcast_to(region[home, k : k + 1, :], (8, width)) for k in range(6)]
        sums = None
        for group in range(width // 8):
            part = source[group * 8 : group * 8 + 8, :]
            x, y, z, charge, sigma, root = [
                jnp.broadcast_to(part[:, k : k + 1], (8, width)) for k in range(6)
            ]
            dx, dy, dz = mine[0] - x, mine[1] - y, mine[2] - z
            softened = jnp.minimum(dx * dx + dy * dy + (dz * dz + soft_core), limit)
            near, four, seven = powers(softened)
            width_pair = mine[4] + sigma
            square = width_pair * width_pair
            sixth = square * square * square
            strength = (mine[5] * root * sixth) * (
                sixth * (seven - seven_at) - (four - four_at)
            ) + (mine[3] * charge) * (near - half)
            pushed = (strength * dx, strength * dy, strength * dz)
            sums = pushed if sums is None else tuple(a + b for a, b in zip(sums, pushed))
        row = pairs[0, index]
        for axis in range(3):
            totals[axis, pl.ds(row, 1), :] += jnp.sum(sums[axis], axis=0, keepdims=True)

    def step(index, carry):
        tile(2 * index)
        tile(2 * index + 1)
        return carry

    lax.fori_loop(0, (count[0] + 1) // 2, step, 0)
    out[...] = totals[:, : out.shape[1], :]


def brick_forces(region, pairs, count, blocks):
    width = region.shape[2]
    return pl.pallas_call(
        force_kernel,
        out_shape=jax.ShapeDtypeStruct((3, blocks, width), jnp.float32),
        in_specs=[
            pl.BlockSpec(memory_space=pltpu.SMEM),
            pl.BlockSpec(memory_space=pltpu.SMEM),
            pl.BlockSpec(memory_space=pltpu.VMEM),
        ],
        out_specs=pl.BlockSpec(memory_space=pltpu.VMEM),
        scratch_shapes=[pltpu.VMEM((3, blocks + 8, width), jnp.float32)],
    )(pairs, count, region)


def rim_shift(length, inner, dtype):
    index = jnp.arange(length + 2, dtype=jnp.int32)
    return ((index == length + 1).astype(jnp.int32) - (index == 0).astype(jnp.int32)).astype(
        dtype
    ) * (inner * cell_edge)


def per_device(coords, charges, atom_types, lj_sigma, lj_epsilon, tile_list):
    span_y = lax.axis_size("gy")
    span_z = lax.axis_size("gz")
    blocks = coords.shape[2]
    width = coords.shape[3]
    layers = blocks // (GRID * GRID)
    ranks = span_y * span_z
    stride = blocks // ranks
    dtype = coords.dtype
    kinds = jnp.arange(lj_sigma.shape[0], dtype=jnp.int32)
    selector = (atom_types[0][:, :, None] == kinds).astype(dtype)
    sigma_atom = jnp.sum(selector * (lj_sigma * sigma_scale), axis=2)
    root_atom = jnp.sum(selector * (jnp.sqrt(lj_epsilon) * root_scale), axis=2)
    rank = lax.axis_index("gy") * span_z + lax.axis_index("gz")
    cell = rank * stride + jnp.arange(blocks, dtype=jnp.int32) // ranks
    corner = [
        (place.astype(dtype) * cell_edge)[:, None]
        for place in (cell // (GRID * layers), cell // layers % GRID, cell % layers)
    ]
    zero = jnp.zeros_like(sigma_atom)
    atoms = jnp.stack(
        [coords[k, 0] + corner[k] for k in range(3)]
        + [charges[0] * charge_scale, sigma_atom, root_atom, zero, zero],
        axis=1,
    )
    outgoing = atoms.reshape(stride, ranks, ROWS, width)
    arrived = lax.all_to_all(outgoing, ("gy", "gz"), split_axis=1, concat_axis=0, tiled=True)
    cells = arrived.reshape(GRID, GRID, layers, ROWS, width)
    padded = extended(cells, (("gx", 0), ("gy", 1), ("gz", 2)), 1)
    shape_pad = (GRID + 2, GRID + 2, layers + 2)
    lines = (
        rim_shift(GRID, GRID, dtype)[:, None, None],
        rim_shift(GRID, GRID, dtype)[None, :, None],
        rim_shift(layers, layers, dtype)[None, None, :],
    )
    axis_row = jnp.arange(ROWS, dtype=jnp.int32)
    shifts = sum(
        jnp.where(axis_row == k, jnp.broadcast_to(line, shape_pad)[..., None], 0.0)
        for k, line in enumerate(lines)
    )
    region = (padded + shifts[..., None]).reshape(-1, ROWS, width)
    pairs = tile_list[0, 0, 0]
    dead = pairs[0] < 0

    def place(ids):
        ids = jnp.maximum(ids, 0)
        slot = ids // blocks
        member = ids % blocks
        px = member // (GRID * layers) + (slot // 9 - 1) * GRID + 1
        py = member // layers % GRID + (slot // 3 % 3 - 1) * GRID + 1
        pz = member % layers + (slot % 3 - 1) * layers + 1
        return jnp.where(dead, 0, (px * (GRID + 2) + py) * (layers + 2) + pz)

    table = jnp.stack(
        [jnp.where(dead, blocks, pairs[0]), place(pairs[0] + 13 * blocks), place(pairs[1])]
    )
    count = jnp.sum((~dead).astype(jnp.int32)).reshape(1)
    totals = brick_forces(region, table, count, blocks)
    sending = totals.reshape(3, ranks, stride, width)[:, :, :, None]
    returned = lax.all_to_all(sending, ("gy", "gz"), split_axis=1, concat_axis=3, tiled=True)
    return returned.reshape(3, 1, blocks, width)


def solution(mesh):
    return jax.shard_map(
        per_device,
        mesh=mesh,
        in_specs=(
            P(None, "gx", ("gy", "gz"), None),
            P("gx", ("gy", "gz"), None),
            P("gx", ("gy", "gz"), None),
            P(),
            P(),
            P("gx", "gy", "gz", None, None),
        ),
        out_specs=P(None, "gx", ("gy", "gz"), None),
        check_vma=False,
    )
```

time: 216 us -> 181 us (0.84)
  other arithmetic: 157 us -> 8.96 us
  Pallas kernels: 0 us -> 74.5 us
  blocking collectives: 7.76 us -> 55.1 us
  local copies, waits for them, and re-layouts: 15.2 us -> 4.01 us
  waiting for transfers between devices: 18.7 us -> 24.4 us
  matrix products: 3.16 us -> 0 us
    reduce_sum x17 -> x2, other arithmetic: 97.2 us -> 3.6 us  [the longest x1 2.89 us: per_device(): root_atom = jnp.sum(selector * (jnp.sqrt(lj_epsilon) * root_scale), axis=2)]
    pallas_call x0 -> x1, Pallas kernels: none -> 74.5 us  [brick_forces(): pl.pallas_call(force_kernel, out_shape=jax.ShapeDtypeStruct((3, blocks, w...]
    select_n x29 -> x1, other arithmetic: 54.6 us -> 0.17 us  [per_device(): jnp.where(dead, blocks, pairs[0])]
    all_to_all x1, blocking collectives: 7.76 us -> 55.1 us  [per_device(): lax.all_to_all(sending, ('gy', 'gz'), split_axis=1, concat_axis=3, tiled=...]
    gather x16 -> x0, local copies, waits for them, and re-layouts: 10.1 us -> none  [the longest x8 5.04 us: advance(): source_block = jnp.take(region, jnp.maximum(pair_ids[1], 0), axis=1)]
    dot_general x8 -> x0, matrix products: 3.16 us -> none  [advance(): jnp.einsum('bg,cga->cba', selector, pushes, precision=lax.Precision.HIGHEST)]
    all_to_all x1, waiting for transfers between devices: 5.15 us -> 8.28 us  [per_device(): lax.all_to_all(outgoing, ('gy', 'gz'), split_axis=1, concat_axis=0, tiled...]
    another operation x5, local copies, waits for them, and re-layouts: 0.24 us -> 2.5 us  [the longest x4 1.56 us: per_device(): jnp.stack([coords[k, 0] + corner[k] for k in range(3)] + [charges[0] * ch...]
where the time goes in v1:
time: 181 us; the launch traced here: 180 us
  Pallas kernels  74.5 us (41%)
  blocking collectives  55.1 us (30%)
  waiting for transfers between devices  24.4 us (13%)
  starting transfers between devices  13.1 us (7%)
  other arithmetic  8.96 us (5%)
  local copies, waits for them, and re-layouts  4.01 us (2%)
    pallas_call x1, Pallas kernels, brick_forces(): pl.pallas_call(force_kernel, out_shape=jax.ShapeDtypeStruct((3, blocks, w...  74.5 us
    all_to_all x1, blocking collectives, per_device(): lax.all_to_all(sending, ('gy', 'gz'), split_axis=1, concat_axis=3, tiled=...  55.1 us
    ppermute x3, waiting for transfers between devices, extended(): lax.ppermute(lax.slice_in_dim(block, block.shape[dim] - width, None, axis...  11 us
    all_to_all x1, waiting for transfers between devices, per_device(): lax.all_to_all(outgoing, ('gy', 'gz'), split_axis=1, concat_axis=0, tiled...  8.28 us
    all_to_all x1, starting transfers between devices, per_device(): lax.all_to_all(outgoing, ('gy', 'gz'), split_axis=1, concat_axis=0, tiled...  5.33 us
    ppermute x3, starting transfers between devices, extended(): lax.ppermute(lax.slice_in_dim(block, 0, width, axis=dim), axis, backward)  5.25 us
    ppermute x3, waiting for transfers between devices, extended(): lax.ppermute(lax.slice_in_dim(block, 0, width, axis=dim), axis, backward)  5.17 us
  transfers between devices with their start and end apart: 7, of which 7 were waited for; matrix products, arithmetic and copies ran while one was open for 1% of the time, Pallas kernels for 0%

profile of v1, /device:TPU:0, one launch (start us, length us, event | category | flops | bytes accessed | tf_op | source)
XLA Modules:
  0.0 180.3 jit_solution(11166446341825424328)
XLA Ops:
  0.1 1.0 bitcast_add_fusion.1
  1.1 0.1 copy.35
  1.2 0.1 copy.36
  1.2 0.1 copy.37
  1.3 0.7 sqrt_multiply_fusion
  2.0 2.9 %select_reduce_fusion = (f32[128,128]{1,0:T(8,128)S(1)}, f32[128,128]{1,0:T(8,128)S(1)}) fusion(f32[64]{0:T(128)S(1)} %get-tuple-element.21, s32[128,128]{1,0:T(8,128)} %bitcast.66, f32[64]{0:T(128)S(1)} %get-tuple-element.22), kind=kLoop, calls=%fused_computation | loop fusion | flops 5210112 | bytes 197120 | tf_op jit(solution)/shard_map/reduce_sum | solution.py:119
  4.9 0.1 copy.39
  5.0 0.1 copy.40
  5.1 0.8 multiply_bitcast_fusion
  5.9 0.1 copy.38
  6.0 1.4 stack.26
  7.4 0.0 copy-start
  7.4 5.3 %all-to-all-start = ((f32[16,8,8,128]{3,2,0,1:T(8,128)}), f32[16,8,8,128]{3,2,0,1:T(8,128)S(1)}, u32[]{:S(2)}, u32[]{:S(2)}) async-start(f32[16,8,8,128]{3,2,0,1:T(8,128)} %stack.26), calls=%async_computation | async-start | bytes 1048576 | tf_op jit(solution)/shard_map/all_to_all | solution.py:133
  12.7 0.1 broadcast_in_dim.64
  12.8 0.1 broadcast_in_dim.65
  12.9 0.1 broadcast_in_dim.69
  13.0 0.1 broadcast_in_dim.70
  13.1 0.1 broadcast_in_dim.74
  13.3 8.3 %all-to-all-done = f32[16,8,8,128]{3,2,0,1:T(8,128)S(1)} async-done(((f32[16,8,8,128]{3,2,0,1:T(8,128)}), f32[16,8,8,128]{3,2,0,1:T(8,128)S(1)}, u32[]{:S(2)}, u32[]{:S(2)}) %all-to-all-start) | async-done | bytes 524320 | tf_op jit(solution)/shard_map/all_to_all | solution.py:133
  21.6 1.6 collective-permute-start
  23.2 2.2 %collective-permute-start.1 = (f32[1,4,8,8,128]{4,3,2,1,0:T(8,128)S(1)}, f32[1,4,8,8,128]{4,3,2,1,0:T(8,128)S(1)}, u32[]{:S(2)}, u32[]{:S(2)}) collective-permute-start(f32[1,4,8,8,128]{4,3,2,1,0:T(8,128)S(1)} %bitcast.64), channel_id=1, source_target_pairs={{8,0},{16,8},{24,16},{0,24},{9,1},{17,9},{25,17},{1,25},{10,2},{18... | collective-permute-start | bytes 393224 | tf_op jit(solution)/shard_map/ppermute | solution.py:32
  25.5 0.2 select_add_fusion
  25.7 4.1 %collective-permute-done = f32[1,4,8,8,128]{4,3,2,1,0:T(8,128)S(1)} collective-permute-done((f32[1,4,8,8,128]{4,3,2,1,0:T(8,128)S(1)}, f32[1,4,8,8,128]{4,3,2,1,0:T(8,128)S(1)}, u32[]{:S(2)}, u32[]{:S(2)}) %collective-permute-start) | collective-permute-done | bytes 131104 | tf_op jit(solution)/shard_map/ppermute | solution.py:29
  29.8 1.4 collective-permute-done.1
  31.2 0.1 collective-permute-start.2
  31.3 1.7 collective-permute-start.3
  33.0 0.0 copy-done
  33.0 0.2 compare_select_fusion.6
  33.2 3.5 %collective-permute-done.2 = f32[6,1,8,8,128]{4,3,2,1,0:T(8,128)S(1)} collective-permute-done((f32[6,1,8,8,128]{4,3,2,1,0:T(8,128)S(1)}, f32[6,1,8,8,128]{4,3,2,1,0:T(8,128)S(1)}, u32[]{:S(2)}, u32[]{:S(2)}) %collective-permute-start.2) | collective-permute-done | bytes 196640 | tf_op jit(solution)/shard_map/ppermute | solution.py:29
  36.7 0.8 collective-permute-done.3
  37.5 0.8 collective-permute-start.4
  38.3 1.3 collective-permute-start.5
  39.6 0.6 pad_add_fusion.pairs
  40.2 0.7 fusion.29
  40.9 3.4 %collective-permute-done.4 = f32[6,6,1,8,128]{4,3,2,1,0:T(8,128)S(1)} collective-permute-done((f32[6,6,1,8,128]{4,3,2,1,0:T(8,128)S(1)}, f32[6,6,1,8,128]{4,3,2,1,0:T(8,128)S(1)}, u32[]{:S(2)}, u32[]{:S(2)}) %collective-permute-start.4) | collective-permute-done | bytes 147488 | tf_op jit(solution)/shard_map/ppermute | solution.py:29
  44.3 3.0 %collective-permute-done.5 = f32[6,6,1,8,128]{4,3,2,1,0:T(8,128)S(1)} collective-permute-done((f32[6,6,1,8,128]{4,3,2,1,0:T(8,128)S(1)}, f32[6,6,1,8,128]{4,3,2,1,0:T(8,128)S(1)}, u32[]{:S(2)}, u32[]{:S(2)}) %collective-permute-start.5) | collective-permute-done | bytes 147488 | tf_op jit(solution)/shard_map/ppermute | solution.py:32
  47.3 0.1 pad_maximum_fusion
  47.4 1.6 bitcast_add_fusion.region
  49.0 74.5 %shard_map.64 = f32[3,128,128]{2,1,0:T(8,128)} custom-call(s32[3,512]{1,0:T(4,128)} %pad_add_fusion.pairs, s32[1]{0:T(128)} %bitcast.4.count, f32[360,8,128]{2,1,0:T(8,128)} %bitcast_add_fusion.region), custom_call_target="tpu_custom_call" | custom-call | tf_op jit(solution)/shard_map/pallas_call | solution.py:87
  123.5 0.9 copy.41
  124.4 55.1 %all_to_all.30 = f32[3,8,16,1,128]{4,2,0,3,1:T(8,128)S(1)} all-to-all(f32[3,8,16,1,128]{4,2,0,3,1:T(8,128)S(1)} %copy.41), channel_id=1, replica_groups=mesh['gx'=4,'gy'=4,'gz'=2] {'gy','gz'}, dimensions={1} | all-to-all | bytes 393216 | tf_op jit(solution)/shard_map/all_to_all | solution.py:166
  179.5 0.7 copy.45
  (11 shorter events, 0.2 us)
Async XLA Ops:
  7.4 25.6 %copy-start = (s32[1,1,1,2,512]{4,3,2,1,0:T(2,128)S(1)}, s32[1,1,1,2,512]{4,3,2,1,0:T(2,128)}, u32[]{:S(2)}) copy-start(s32[1,1,1,2,512]{4,3,2,1,0:T(2,128)} %param.11) | copy-start | bytes 12292
  7.4 14.1 %all-to-all-start = ((f32[16,8,8,128]{3,2,0,1:T(8,128)}), f32[16,8,8,128]{3,2,0,1:T(8,128)S(1)}, u32[]{:S(2)}, u32[]{:S(2)}) async-start(f32[16,8,8,128]{3,2,0,1:T(8,128)} %stack.26), calls=%async_computation | async-start | bytes 1048576 | tf_op jit(solution)/shard_map/all_to_all | solution.py:133
  21.6 8.2 %collective-permute-start = (f32[1,4,8,8,128]{4,3,2,1,0:T(8,128)S(1)}, f32[1,4,8,8,128]{4,3,2,1,0:T(8,128)S(1)}, u32[]{:S(2)}, u32[]{:S(2)}) collective-permute-start(f32[1,4,8,8,128]{4,3,2,1,0:T(8,128)S(1)} %bitcast.65), channel_id=1, source_target_pairs={{0,8},{8,16},{16,24},{24,0},{1,9},{9,17},{17,25},{25,1},{2,10},{10... | collective-permute-start | bytes 393224 | tf_op jit(solution)/shard_map/ppermute | solution.py:29
  23.2 8.0 %collective-permute-start.1 = (f32[1,4,8,8,128]{4,3,2,1,0:T(8,128)S(1)}, f32[1,4,8,8,128]{4,3,2,1,0:T(8,128)S(1)}, u32[]{:S(2)}, u32[]{:S(2)}) collective-permute-start(f32[1,4,8,8,128]{4,3,2,1,0:T(8,128)S(1)} %bitcast.64), channel_id=1, source_target_pairs={{8,0},{16,8},{24,16},{0,24},{9,1},{17,9},{25,17},{1,25},{10,2},{18... | collective-permute-start | bytes 393224 | tf_op jit(solution)/shard_map/ppermute | solution.py:32
  31.2 5.5 %collective-permute-start.2 = (f32[6,1,8,8,128]{4,3,2,1,0:T(8,128)S(1)}, f32[6,1,8,8,128]{4,3,2,1,0:T(8,128)S(1)}, u32[]{:S(2)}, u32[]{:S(2)}) collective-permute-start(f32[6,1,8,8,128]{4,3,2,1,0:T(8,128)S(1)} %get-tuple-element.9), channel_id=1, source_target_pairs={{0,2},{2,4},{4,6},{6,0},{1,3},{3,5},{5,7},{7,1},{8,10},{10,12},{12... | collective-permute-start | bytes 589832 | tf_op jit(solution)/shard_map/ppermute | solution.py:29
  31.3 6.2 %collective-permute-start.3 = (f32[6,1,8,8,128]{4,3,2,1,0:T(8,128)S(1)}, f32[6,1,8,8,128]{4,3,2,1,0:T(8,128)S(1)}, u32[]{:S(2)}, u32[]{:S(2)}) collective-permute-start(f32[6,1,8,8,128]{4,3,2,1,0:T(8,128)S(1)} %get-tuple-element.10), channel_id=1, source_target_pairs={{2,0},{4,2},{6,4},{0,6},{3,1},{5,3},{7,5},{1,7},{10,8},{12,10},{14... | collective-permute-start | bytes 589832 | tf_op jit(solution)/shard_map/ppermute | solution.py:32
  37.5 6.8 %collective-permute-start.4 = (f32[6,6,1,8,128]{4,3,2,1,0:T(8,128)S(1)}, f32[6,6,1,8,128]{4,3,2,1,0:T(8,128)S(1)}, u32[]{:S(2)}, u32[]{:S(2)}) collective-permute-start(f32[6,6,1,8,128]{4,3,2,1,0:T(8,128)S(1)} %get-tuple-element.7), channel_id=1, source_target_pairs={{0,1},{1,0},{2,3},{3,2},{4,5},{5,4},{6,7},{7,6},{8,9},{9,8},{10,11... | collective-permute-start | bytes 442376 | tf_op jit(solution)/shard_map/ppermute | solution.py:29
  38.3 9.0 %collective-permute-start.5 = (f32[6,6,1,8,128]{4,3,2,1,0:T(8,128)S(1)}, f32[6,6,1,8,128]{4,3,2,1,0:T(8,128)S(1)}, u32[]{:S(2)}, u32[]{:S(2)}) collective-permute-start(f32[6,6,1,8,128]{4,3,2,1,0:T(8,128)S(1)} %get-tuple-element.8), channel_id=1, source_target_pairs={{1,0},{0,1},{3,2},{2,3},{5,4},{4,5},{7,6},{6,7},{9,8},{8,9},{11,10... | collective-permute-start | bytes 442376 | tf_op jit(solution)/shard_map/ppermute | solution.py:32

commit v2 on v1

v2 whole, which is shorter than its diff:
```python
import functools

import jax
import jax.numpy as jnp
from jax import lax
from jax.experimental import pallas as pl
from jax.experimental.pallas import tpu as pltpu
from jax.sharding import PartitionSpec as P

GRID = 4
ROWS = 8
BATCH = 4

cell_edge = 11.0
cutoff = 9.0
soft_core = 16.0
coulomb = 332.0636
limit = cutoff * cutoff + soft_core
sigma_scale = 0.5 * 2.0 ** (1.0 / 6.0)
root_scale = 12.0**0.5
charge_scale = coulomb**0.5


def extended(block, sides, width):
    for axis, dim in sides:
        count = lax.axis_size(axis)
        forward = [(i, i + 1) for i in range(count - 1)]
        forward.append((count - 1, 0))
        backward = [(target, source) for source, target in forward]
        low = lax.ppermute(
            lax.slice_in_dim(block, block.shape[dim] - width, None, axis=dim), axis, forward
        )
        high = lax.ppermute(lax.slice_in_dim(block, 0, width, axis=dim), axis, backward)
        block = jnp.concatenate([low, block, high], axis=dim)
    return block


def powers(softened):
    root = lax.rsqrt(softened)
    one = root * root
    two = one * one
    four = two * two
    return one * root, four, four * (two * one)


def split(value):
    high = value.astype(jnp.bfloat16).astype(jnp.float32)
    rest = value - high
    middle = rest.astype(jnp.bfloat16).astype(jnp.float32)
    return high, middle, rest - middle


def stacked(parts):
    return jnp.concatenate(parts, axis=0).astype(jnp.bfloat16)


def source_stack(source):
    high, middle, low = split(source)
    return stacked([high, middle, high, middle, high, low])


def home_stack(home):
    high, middle, low = split(home)
    return stacked([high, high, middle, middle, low, high])


def moved_home(pairs, index, region):
    home = region[pairs[1, index]]
    lane_row = lax.broadcasted_iota(jnp.int32, home.shape, 0)
    step = [pairs[3 + k, index].astype(jnp.float32) * cell_edge for k in range(3)]
    offset = jnp.where(
        lane_row == 0, step[0], jnp.where(lane_row == 1, step[1], jnp.where(lane_row == 2, step[2], 0.0))
    )
    return home, home - offset, lane_row


def pair_terms(pairs, index, region, terms):
    home, moved, lane_row = moved_home(pairs, index, region)
    square = jnp.sum(jnp.where(lane_row < 3, moved * moved, 0.0), axis=0, keepdims=True)
    ones = jnp.where(lane_row == 4, 1.0, 0.0)
    distance = jnp.where(lane_row < 3, -2.0 * moved, jnp.where(lane_row == 3, square, ones))
    sigma = jnp.where(lane_row == 3, home[5:6, :], jnp.where(lane_row == 5, 1.0, 0.0))
    root = jnp.where(lane_row == 6, home, 0.0)
    charge = jnp.where(lane_row == 7, home, 0.0)
    wide = jnp.concatenate([distance, sigma, root, charge], axis=1)
    terms[...] = lax.dot_general(
        source_stack(region[pairs[2, index]]),
        home_stack(wide),
        (((0,), (0,)), ((), ())),
        preferred_element_type=jnp.float32,
    )


def strengths(terms, high, low, at_limit):
    width = terms.shape[0]
    near_at, four_at, seven_at = at_limit
    for start in range(0, width, 16):
        rows = pl.ds(start, 16)
        softened, sigma, root, charge = [
            terms[rows, k * width : (k + 1) * width] for k in range(4)
        ]
        near, four, seven = powers(jnp.minimum(softened, limit))
        square = sigma * sigma
        sixth = square * square * square
        strength = (root * sixth) * (
            sixth * (seven - seven_at) - (four - four_at)
        ) + charge * (near - near_at)
        top = strength.astype(jnp.bfloat16)
        high[rows, :] = top
        low[rows, :] = (strength - top.astype(jnp.float32)).astype(jnp.bfloat16)


def add_forces(pairs, index, region, high, low, totals):
    _, moved, _ = moved_home(pairs, index, region)
    top, middle, _ = split(region[pairs[2, index]])
    weights = stacked([top, middle])
    both = jnp.dot(weights, high[...], preferred_element_type=jnp.float32) + jnp.dot(
        weights, low[...], preferred_element_type=jnp.float32
    )
    summed = both[:ROWS] + both[ROWS:]
    totals[pairs[0, index]] += moved * summed[3:4, :] - summed


def force_kernel(pairs, count, region, out, totals, *slots):
    width = region.shape[2]
    at_limit = powers(jnp.full((16, width), limit, jnp.float32))
    totals[...] = jnp.zeros_like(totals)
    terms = (slots[:BATCH], slots[BATCH : 2 * BATCH])
    highs = (slots[2 * BATCH : 3 * BATCH], slots[3 * BATCH : 4 * BATCH])
    lows = (slots[4 * BATCH : 5 * BATCH], slots[5 * BATCH :])

    def step(index, carry):
        for turn in range(2):
            first = (2 * index + turn) * BATCH
            for t in range(BATCH):
                add_forces(pairs, first + t, region, highs[turn][t], lows[turn][t], totals)
                strengths(terms[1 - turn][t], highs[1 - turn][t], lows[1 - turn][t], at_limit)
                pair_terms(pairs, first + 2 * BATCH + t, region, terms[turn][t])
        return carry

    groups = (count[0] + BATCH - 1) // BATCH
    lax.fori_loop(0, (groups + 3) // 2, step, 0)
    for axis in range(3):
        out[axis] = totals[: out.shape[1], axis, :]


def brick_forces(region, pairs, count, blocks):
    width = region.shape[2]
    return pl.pallas_call(
        force_kernel,
        out_shape=jax.ShapeDtypeStruct((3, blocks, width), jnp.float32),
        in_specs=[
            pl.BlockSpec(memory_space=pltpu.SMEM),
            pl.BlockSpec(memory_space=pltpu.SMEM),
            pl.BlockSpec(memory_space=pltpu.VMEM),
        ],
        out_specs=pl.BlockSpec(memory_space=pltpu.VMEM),
        scratch_shapes=[pltpu.VMEM((blocks + 1, ROWS, width), jnp.float32)]
        + [pltpu.VMEM((width, 4 * width), jnp.float32)] * (2 * BATCH)
        + [pltpu.VMEM((width, width), jnp.bfloat16)] * (4 * BATCH),
    )(pairs, count, region)


def per_device(coords, charges, atom_types, lj_sigma, lj_epsilon, tile_list):
    span_y = lax.axis_size("gy")
    span_z = lax.axis_size("gz")
    blocks = coords.shape[2]
    width = coords.shape[3]
    layers = blocks // (GRID * GRID)
    ranks = span_y * span_z
    stride = blocks // ranks
    dtype = coords.dtype
    kinds = jnp.arange(lj_sigma.shape[0], dtype=jnp.int32)
    selector = (atom_types[0][:, :, None] == kinds).astype(dtype)
    sigma_atom = jnp.sum(selector * (lj_sigma * sigma_scale), axis=2)
    root_atom = jnp.sum(selector * (jnp.sqrt(lj_epsilon) * root_scale), axis=2)
    inner = coords[:, 0] - 0.5 * cell_edge
    square = inner[0] * inner[0] + inner[1] * inner[1] + inner[2] * inner[2] + soft_core
    atoms = jnp.stack(
        [inner[0], inner[1], inner[2], jnp.ones_like(square), square]
        + [sigma_atom, root_atom, charges[0] * charge_scale],
        axis=1,
    )
    outgoing = atoms.reshape(stride, ranks, ROWS, width)
    arrived = lax.all_to_all(outgoing, ("gy", "gz"), split_axis=1, concat_axis=0, tiled=True)
    cells = arrived.reshape(GRID, GRID, layers, ROWS, width)
    padded = extended(cells, (("gx", 0), ("gy", 1), ("gz", 2)), 1)
    region = padded.reshape(-1, ROWS, width)
    pairs = jnp.pad(
        tile_list[0, 0, 0], ((0, 0), (2 * BATCH, 4 * BATCH)), constant_values=-1
    )
    dead = pairs[0] < 0

    def place(ids):
        slot = ids // blocks
        member = ids % blocks
        px = member // (GRID * layers) + (slot // 9 - 1) * GRID
        py = member // layers % GRID + (slot // 3 % 3 - 1) * GRID
        pz = member % layers + (slot % 3 - 1) * layers
        return px, py, pz

    own = place(jnp.where(dead, 0, pairs[0]) + 13 * blocks)
    other = place(jnp.where(dead, 13 * blocks, pairs[1]))
    lines = [
        ((x + 1) * (GRID + 2) + y + 1) * (layers + 2) + z + 1 for x, y, z in (own, other)
    ]
    table = jnp.stack(
        [jnp.where(dead, blocks, pairs[0])] + lines + [b - a for a, b in zip(own, other)]
    )
    count = jnp.sum((~dead).astype(jnp.int32)).reshape(1)
    totals = brick_forces(region, table, count, blocks)
    sending = totals.reshape(3, ranks, stride, width)[:, :, :, None]
    returned = lax.all_to_all(sending, ("gy", "gz"), split_axis=1, concat_axis=3, tiled=True)
    return returned.reshape(3, 1, blocks, width)


def solution(mesh):
    return jax.shard_map(
        per_device,
        mesh=mesh,
        in_specs=(
            P(None, "gx", ("gy", "gz"), None),
            P("gx", ("gy", "gz"), None),
            P("gx", ("gy", "gz"), None),
            P(),
            P(),
            P("gx", "gy", "gz", None, None),
        ),
        out_specs=P(None, "gx", ("gy", "gz"), None),
        check_vma=False,
    )
```

time: 181 us -> 113 us (0.62)
  the two profiles are of different devices: /device:TPU:0 before, /device:TPU:9 now
where the time goes in v2:
time: 113 us; the launch traced here: 112 us
  blocking collectives  34.3 us (30%)
  Pallas kernels  31.3 us (28%)
  waiting for transfers between devices  27.1 us (24%)
  starting transfers between devices  9.08 us (8%)
  other arithmetic  6.9 us (6%)
  local copies, waits for them, and re-layouts  3.43 us (3%)
    all_to_all x1, blocking collectives, per_device(): lax.all_to_all(sending, ('gy', 'gz'), split_axis=1, concat_axis=3, tiled=...  34.3 us
    pallas_call x1, Pallas kernels, brick_forces(): pl.pallas_call(force_kernel, out_shape=jax.ShapeDtypeStruct((3, blocks, w...  31.3 us
    ppermute x3, waiting for transfers between devices, extended(): lax.ppermute(lax.slice_in_dim(block, block.shape[dim] - width, None, axis...  10.3 us
    ppermute x3, waiting for transfers between devices, extended(): lax.ppermute(lax.slice_in_dim(block, 0, width, axis=dim), axis, backward)  9.19 us
    all_to_all x1, waiting for transfers between devices, per_device(): lax.all_to_all(outgoing, ('gy', 'gz'), split_axis=1, concat_axis=0, tiled...  7.57 us
    all_to_all x1, starting transfers between devices, per_device(): lax.all_to_all(outgoing, ('gy', 'gz'), split_axis=1, concat_axis=0, tiled...  4.39 us
    ppermute x3, starting transfers between devices, extended(): lax.ppermute(lax.slice_in_dim(block, block.shape[dim] - width, None, axis...  3.74 us
    reduce_sum x1, other arithmetic, per_device(): root_atom = jnp.sum(selector * (jnp.sqrt(lj_epsilon) * root_scale), axis=2)  2.89 us
  transfers between devices with their start and end apart: 7, of which 7 were waited for; matrix products, arithmetic and copies ran while one was open for 1% of the time, Pallas kernels for 0%

profile of v2, /device:TPU:9, one launch (start us, length us, event | category | flops | bytes accessed | tf_op | source)
XLA Modules:
  0.0 112.3 jit_solution(3013345580902680883)
XLA Ops:
  0.0 0.0 copy-start
  0.0 1.0 broadcast_add_fusion
  1.0 0.0 copy-start.1
  1.1 0.7 sqrt_multiply_fusion
  1.8 2.9 %select_reduce_fusion = (f32[128,128]{1,0:T(8,128)S(1)}, f32[128,128]{1,0:T(8,128)S(1)}) fusion(f32[64]{0:T(128)S(1)} %get-tuple-element.38, s32[128,128]{1,0:T(8,128)} %bitcast.54, f32[64]{0:T(128)S(1)} %get-tuple-element.39), kind=kLoop, calls=%fused_computation | loop fusion | flops 5210112 | bytes 197120 | tf_op jit(solution)/shard_map/reduce_sum | solution.py:176
  4.7 0.0 copy-done
  4.7 0.9 copy.17
  5.6 4.4 %all-to-all-start = ((f32[16,8,8,128]{3,0,2,1:T(8,128)}), f32[16,8,8,128]{3,0,2,1:T(8,128)S(1)}, u32[]{:S(2)}, u32[]{:S(2)}) async-start(f32[16,8,8,128]{3,0,2,1:T(8,128)} %copy.17), calls=%async_computation | async-start | bytes 1048576 | tf_op jit(solution)/shard_map/all_to_all | solution.py:185
  10.0 0.0 copy-done.1
  10.0 0.8 fusion.18
  10.8 7.6 %all-to-all-done = f32[16,8,8,128]{3,0,2,1:T(8,128)S(1)} async-done(((f32[16,8,8,128]{3,0,2,1:T(8,128)}), f32[16,8,8,128]{3,0,2,1:T(8,128)S(1)}, u32[]{:S(2)}, u32[]{:S(2)}) %all-to-all-start) | async-done | bytes 524320 | tf_op jit(solution)/shard_map/all_to_all | solution.py:185
  18.3 0.2 copy.26
  18.5 1.3 %collective-permute-start = (f32[1,4,8,8,128]{4,3,2,1,0:T(8,128)S(1)}, f32[1,4,8,8,128]{4,3,2,1,0:T(8,128)S(1)}, u32[]{:S(2)}, u32[]{:S(2)}) collective-permute-start(f32[1,4,8,8,128]{4,3,2,1,0:T(8,128)S(1)} %bitcast.53), channel_id=1, source_target_pairs={{0,8},{8,16},{16,24},{24,0},{1,9},{9,17},{17,25},{25,1},{2,10},{10... | collective-permute-start | bytes 393224 | tf_op jit(solution)/shard_map/ppermute | solution.py:30
  19.9 0.2 collective-permute-start.1
  20.0 0.1 fusion.19
  20.2 3.0 %collective-permute-done = f32[1,4,8,8,128]{4,3,2,1,0:T(8,128)S(1)} collective-permute-done((f32[1,4,8,8,128]{4,3,2,1,0:T(8,128)S(1)}, f32[1,4,8,8,128]{4,3,2,1,0:T(8,128)S(1)}, u32[]{:S(2)}, u32[]{:S(2)}) %collective-permute-start) | collective-permute-done | bytes 131104 | tf_op jit(solution)/shard_map/ppermute | solution.py:30
  23.2 4.5 %collective-permute-done.1 = f32[1,4,8,8,128]{4,3,2,1,0:T(8,128)S(1)} collective-permute-done((f32[1,4,8,8,128]{4,3,2,1,0:T(8,128)S(1)}, f32[1,4,8,8,128]{4,3,2,1,0:T(8,128)S(1)}, u32[]{:S(2)}, u32[]{:S(2)}) %collective-permute-start.1) | collective-permute-done | bytes 131104 | tf_op jit(solution)/shard_map/ppermute | solution.py:33
  27.7 1.6 %collective-permute-start.2 = (f32[6,1,8,8,128]{4,3,2,1,0:T(8,128)S(1)}, f32[6,1,8,8,128]{4,3,2,1,0:T(8,128)S(1)}, u32[]{:S(2)}, u32[]{:S(2)}) collective-permute-start(f32[6,1,8,8,128]{4,3,2,1,0:T(8,128)S(1)} %get-tuple-element.24), channel_id=1, source_target_pairs={{0,2},{2,4},{4,6},{6,0},{1,3},{3,5},{5,7},{7,1},{8,10},{10,12},{12... | collective-permute-start | bytes 589832 | tf_op jit(solution)/shard_map/ppermute | solution.py:30
  29.3 0.0 collective-permute-start.3
  29.3 0.1 fusion.25
  29.5 3.7 %collective-permute-done.2 = f32[6,1,8,8,128]{4,3,2,1,0:T(8,128)S(1)} collective-permute-done((f32[6,1,8,8,128]{4,3,2,1,0:T(8,128)S(1)}, f32[6,1,8,8,128]{4,3,2,1,0:T(8,128)S(1)}, u32[]{:S(2)}, u32[]{:S(2)}) %collective-permute-start.2) | collective-permute-done | bytes 196640 | tf_op jit(solution)/shard_map/ppermute | solution.py:30
  33.2 1.5 %collective-permute-done.3 = f32[6,1,8,8,128]{4,3,2,1,0:T(8,128)S(1)} collective-permute-done((f32[6,1,8,8,128]{4,3,2,1,0:T(8,128)S(1)}, f32[6,1,8,8,128]{4,3,2,1,0:T(8,128)S(1)}, u32[]{:S(2)}, u32[]{:S(2)}) %collective-permute-start.3) | collective-permute-done | bytes 196640 | tf_op jit(solution)/shard_map/ppermute | solution.py:33
  34.8 0.8 collective-permute-start.4
  35.5 0.8 collective-permute-start.5
  36.3 0.6 stack.26.pairs
  37.0 3.6 %collective-permute-done.4 = f32[6,6,1,8,128]{4,3,2,1,0:T(8,128)S(1)} collective-permute-done((f32[6,6,1,8,128]{4,3,2,1,0:T(8,128)S(1)}, f32[6,6,1,8,128]{4,3,2,1,0:T(8,128)S(1)}, u32[]{:S(2)}, u32[]{:S(2)}) %collective-permute-start.4) | collective-permute-done | bytes 147488 | tf_op jit(solution)/shard_map/ppermute | solution.py:30
  40.6 3.2 %collective-permute-done.5 = f32[6,6,1,8,128]{4,3,2,1,0:T(8,128)S(1)} collective-permute-done((f32[6,6,1,8,128]{4,3,2,1,0:T(8,128)S(1)}, f32[6,6,1,8,128]{4,3,2,1,0:T(8,128)S(1)}, u32[]{:S(2)}, u32[]{:S(2)}) %collective-permute-start.5) | collective-permute-done | bytes 147488 | tf_op jit(solution)/shard_map/ppermute | solution.py:33
  43.7 1.2 %pad_maximum_fusion = f32[6,6,10,8,128]{4,3,2,1,0:T(8,128)} fusion(f32[6,6,1,8,128]{4,3,2,1,0:T(8,128)S(1)} %collective-permute-done.5, f32[6,1,8,8,128]{4,3,2,1,0:T(8,128)S(1)} %collective-permute-done.3, f32[1,4,8,8,128]{4,3,2,1,0:T(8,128)S(1)} %collective-permute-done.1, f32[4,4,8,8,128]{4,3,2,1,0:T(8,128)S(1)} %bitcast.49, ...), kind=kLoop, calls=%fused_computation.3 | loop fusion | flops 2211840 | bytes 2949120 | tf_op jit(solution)/shard_map/concatenate | solution.py:34
  45.0 31.3 %shard_map.64 = f32[3,128,128]{2,1,0:T(8,128)} custom-call(s32[6,536]{1,0:T(8,128)} %stack.26.pairs, s32[1]{0:T(128)} %bitcast.1.count, f32[360,8,128]{2,1,0:T(8,128)} %bitcast.50), custom_call_target="tpu_custom_call" | custom-call | tf_op jit(solution)/shard_map/pallas_call | solution.py:149
  76.3 0.9 copy.19
  77.2 34.3 %all_to_all.30 = f32[3,8,16,1,128]{4,2,0,3,1:T(8,128)S(1)} all-to-all(f32[3,8,16,1,128]{4,2,0,3,1:T(8,128)S(1)} %copy.19), channel_id=1, replica_groups=mesh['gx'=4,'gy'=4,'gz'=2] {'gy','gz'}, dimensions={1} | all-to-all | bytes 393216 | tf_op jit(solution)/shard_map/all_to_all | solution.py:213
  111.6 0.7 copy.25
  (12 shorter events, 0.2 us)
Async XLA Ops:
  0.0 4.7 %copy-start = (f32[1,128,128]{2,1,0:T(8,128)S(1)}, f32[1,128,128]{2,1,0:T(8,128)}, u32[]{:S(2)}) copy-start(f32[1,128,128]{2,1,0:T(8,128)} %param.7) | copy-start | bytes 196612
  1.0 9.0 %copy-start.1 = (s32[1,1,1,2,512]{4,3,2,1,0:T(2,128)S(1)}, s32[1,1,1,2,512]{4,3,2,1,0:T(2,128)}, u32[]{:S(2)}) copy-start(s32[1,1,1,2,512]{4,3,2,1,0:T(2,128)} %param.11) | copy-start | bytes 12292
  5.6 12.7 %all-to-all-start = ((f32[16,8,8,128]{3,0,2,1:T(8,128)}), f32[16,8,8,128]{3,0,2,1:T(8,128)S(1)}, u32[]{:S(2)}, u32[]{:S(2)}) async-start(f32[16,8,8,128]{3,0,2,1:T(8,128)} %copy.17), calls=%async_computation | async-start | bytes 1048576 | tf_op jit(solution)/shard_map/all_to_all | solution.py:185
  18.5 4.6 %collective-permute-start = (f32[1,4,8,8,128]{4,3,2,1,0:T(8,128)S(1)}, f32[1,4,8,8,128]{4,3,2,1,0:T(8,128)S(1)}, u32[]{:S(2)}, u32[]{:S(2)}) collective-permute-start(f32[1,4,8,8,128]{4,3,2,1,0:T(8,128)S(1)} %bitcast.53), channel_id=1, source_target_pairs={{0,8},{8,16},{16,24},{24,0},{1,9},{9,17},{17,25},{25,1},{2,10},{10... | collective-permute-start | bytes 393224 | tf_op jit(solution)/shard_map/ppermute | solution.py:30
  19.9 7.8 %collective-permute-start.1 = (f32[1,4,8,8,128]{4,3,2,1,0:T(8,128)S(1)}, f32[1,4,8,8,128]{4,3,2,1,0:T(8,128)S(1)}, u32[]{:S(2)}, u32[]{:S(2)}) collective-permute-start(f32[1,4,8,8,128]{4,3,2,1,0:T(8,128)S(1)} %bitcast.52), channel_id=1, source_target_pairs={{8,0},{16,8},{24,16},{0,24},{9,1},{17,9},{25,17},{1,25},{10,2},{18... | collective-permute-start | bytes 393224 | tf_op jit(solution)/shard_map/ppermute | solution.py:33
  27.7 5.5 %collective-permute-start.2 = (f32[6,1,8,8,128]{4,3,2,1,0:T(8,128)S(1)}, f32[6,1,8,8,128]{4,3,2,1,0:T(8,128)S(1)}, u32[]{:S(2)}, u32[]{:S(2)}) collective-permute-start(f32[6,1,8,8,128]{4,3,2,1,0:T(8,128)S(1)} %get-tuple-element.24), channel_id=1, source_target_pairs={{0,2},{2,4},{4,6},{6,0},{1,3},{3,5},{5,7},{7,1},{8,10},{10,12},{12... | collective-permute-start | bytes 589832 | tf_op jit(solution)/shard_map/ppermute | solution.py:30
  29.3 5.4 %collective-permute-start.3 = (f32[6,1,8,8,128]{4,3,2,1,0:T(8,128)S(1)}, f32[6,1,8,8,128]{4,3,2,1,0:T(8,128)S(1)}, u32[]{:S(2)}, u32[]{:S(2)}) collective-permute-start(f32[6,1,8,8,128]{4,3,2,1,0:T(8,128)S(1)} %get-tuple-element.25), channel_id=1, source_target_pairs={{2,0},{4,2},{6,4},{0,6},{3,1},{5,3},{7,5},{1,7},{10,8},{12,10},{14... | collective-permute-start | bytes 589832 | tf_op jit(solution)/shard_map/ppermute | solution.py:33
  34.8 5.8 %collective-permute-start.4 = (f32[6,6,1,8,128]{4,3,2,1,0:T(8,128)S(1)}, f32[6,6,1,8,128]{4,3,2,1,0:T(8,128)S(1)}, u32[]{:S(2)}, u32[]{:S(2)}) collective-permute-start(f32[6,6,1,8,128]{4,3,2,1,0:T(8,128)S(1)} %get-tuple-element.22), channel_id=1, source_target_pairs={{0,1},{1,0},{2,3},{3,2},{4,5},{5,4},{6,7},{7,6},{8,9},{9,8},{10,11... | collective-permute-start | bytes 442376 | tf_op jit(solution)/shard_map/ppermute | solution.py:30
  35.5 8.2 %collective-permute-start.5 = (f32[6,6,1,8,128]{4,3,2,1,0:T(8,128)S(1)}, f32[6,6,1,8,128]{4,3,2,1,0:T(8,128)S(1)}, u32[]{:S(2)}, u32[]{:S(2)}) collective-permute-start(f32[6,6,1,8,128]{4,3,2,1,0:T(8,128)S(1)} %get-tuple-element.23), channel_id=1, source_target_pairs={{1,0},{0,1},{3,2},{2,3},{5,4},{4,5},{7,6},{6,7},{9,8},{8,9},{11,10... | collective-permute-start | bytes 442376 | tf_op jit(solution)/shard_map/ppermute | solution.py:33
